TPU v7x, 16 devices: a whole 2x2x2 slice. The times are simulated.
16 devices in a mesh: dp: 1, tp: 16 (over x, y, z, core).
Axes of the slice: x: 2, y: 2, z: 2, core: 2. Of those that a mesh axis runs over, the one named last changes fastest.
Arguments:
- x: bfloat16 [2048, 3072], P('dp')
- dy: bfloat16 [2048, 3072], P('dp')
- gate: bfloat16 [2048, 8192], P('dp', 'tp')
- up: bfloat16 [2048, 8192], P('dp', 'tp')
- w_gate: bfloat16 [3072, 8192], P(None, 'tp')
- w_up: bfloat16 [3072, 8192], P(None, 'tp')
- w_down: bfloat16 [8192, 3072], P('tp')
Outputs:
- output 1: bfloat16 [2048, 3072], P('dp')
- output 2: bfloat16 [3072, 8192], P('dp', 'tp')
- output 3: bfloat16 [3072, 8192], P('dp', 'tp')
- output 4: bfloat16 [8192, 3072], P(('dp', 'tp'))
All inputs are finite; a program needn't handle non-finite values.
Results may differ from a plain program's by a relative error of at most 0.012.
Values are sent between devices in bfloat16 or wider.
A program may use at most 2 GiB of HBM per device.

v0:
```python
import jax
import jax.numpy as jnp
from jax import lax
from jax.sharding import PartitionSpec as P


def act(gate, up):
    return jax.nn.silu(gate) * up


def solution(mesh):
    def step(x, dy, gate, up, w_gate, w_up, w_down):
        hidden, back = jax.vjp(act, gate.astype(jnp.float32), up.astype(jnp.float32))
        d_hidden = jnp.dot(dy, w_down.T, preferred_element_type=jnp.float32)
        d_gate, d_up = (g.astype(jnp.bfloat16) for g in back(d_hidden))
        term = jnp.dot(d_gate, w_gate.T, preferred_element_type=jnp.float32) + jnp.dot(d_up, w_up.T, preferred_element_type=jnp.float32)
        dx = lax.psum(term.astype(jnp.bfloat16), "tp")
        dw_gate = jnp.dot(x.T, d_gate, preferred_element_type=jnp.float32)
        dw_up = jnp.dot(x.T, d_up, preferred_element_type=jnp.float32)
        dw_down = jnp.dot(hidden.astype(jnp.bfloat16).T, dy, preferred_element_type=jnp.float32)
        return dx, *(g.astype(jnp.bfloat16) for g in (dw_gate, dw_up, dw_down))

    tokens, columns, rows = P("dp", None), P(None, "tp"), P("tp", None)
    return jax.shard_map(
        step,
        mesh=mesh,
        in_specs=(tokens, tokens, P("dp", "tp"), P("dp", "tp"), columns, columns, rows),
        out_specs=(tokens, P("dp", "tp"), P("dp", "tp"), P(("dp", "tp"), None)),
        check_vma=False,
    )
```

profile of v0, /device:TPU:0, one launch (start us, length us, event | category | flops | bytes accessed | tf_op | source)
XLA Modules:
  0.0 219.5 jit_solution(517707953861111566)
XLA Ops:
  7.2 0.0 copy-start
  7.2 0.0 all-reduce.2.cloned.1.call-start
  7.2 16.1 %fusion.6 = (bf16[2048,512]{1,0:T(8,128)(2,1)S(1)}, f32[2048,512]{1,0:T(8,128)}) fusion(bf16[2048,512]{1,0:T(8,128)(2,1)} %param.9, bf16[2048,512]{1,0:T(8,128)(2,1)} %param.10, bf16[2048,3072]{1,0:T(8,128)(2,1)} %param.8, bf16[512,3072]{1,0:T(8,128)(2,1)} %param.13), kind=kOutput, calls=%fused_computation.16 | convolution fusion | flops 6456082432 | bytes 26214400 | tf_op jit(solution)/shard_map/dot_general | solution.py:14
  23.3 0.0 copy-start.4
  23.3 0.0 copy-done
  23.3 0.0 copy-start.2
  23.3 0.0 copy-start.3
  23.3 12.0 %fusion.11 = f32[2048,3072]{1,0:T(8,128)} fusion(bf16[2048,512]{1,0:T(8,128)(2,1)S(1)} %get-tuple-element.8, bf16[3072,512]{1,0:T(8,128)(2,1)S(1)} %copy-done), kind=kOutput, calls=%fused_computation.21 | convolution fusion | flops 6442450944 | bytes 30408704 | tf_op jit(solution)/shard_map/dot_general | solution.py:16
  35.3 0.0 copy-done.4
  35.3 0.0 copy-done.2
  35.3 0.0 copy-done.3
  35.3 18.7 %add_convert_fusion = bf16[2048,3072]{1,0:T(8,128)(2,1)} fusion(f32[2048,3072]{1,0:T(8,128)} %fusion.11, bf16[3072,512]{1,0:T(8,128)(2,1)S(1)} %copy-done.2, f32[2048,512]{1,0:T(8,128)} %get-tuple-element.9, bf16[2048,512]{1,0:T(8,128)(2,1)S(1)} %copy-done.3), kind=kOutput, calls=%fused_computation | convolution fusion | flops 6462373888 | bytes 47185920 | tf_op jit(solution)/shard_map/dot_general | solution.py:16
  54.0 0.0 all-reduce.2.cloned.1.call-update
  54.0 10.6 %fusion.7 = bf16[3072,512]{0,1:T(8,128)(2,1)S(1)} fusion(bf16[2048,512]{1,0:T(8,128)(2,1)} %copy-done.4, bf16[2048,3072]{1,0:T(8,128)(2,1)} %param.7), kind=kOutput, calls=%fused_computation.18 | convolution fusion | flops 6444023808 | bytes 17825792 | tf_op jit(solution)/shard_map/dot_general | solution.py:18
  64.6 2.8 %copy.11 = bf16[3072,512]{1,0:T(8,128)(2,1)} copy(bf16[3072,512]{0,1:T(8,128)(2,1)S(1)} %fusion.7) | data formatting | bytes 6291456
  67.4 13.0 %fusion.8 = bf16[3072,512]{0,1:T(8,128)(2,1)S(1)} fusion(bf16[2048,3072]{1,0:T(8,128)(2,1)} %param.7, f32[2048,512]{1,0:T(8,128)} %get-tuple-element.9, bf16[2048,512]{1,0:T(8,128)(2,1)} %param.9), kind=kOutput, calls=%fused_computation.19 | convolution fusion | flops 6451363840 | bytes 22020096 | tf_op jit(solution)/shard_map/dot_general | solution.py:19
  80.4 2.8 %copy.12 = bf16[3072,512]{1,0:T(8,128)(2,1)} copy(bf16[3072,512]{0,1:T(8,128)(2,1)S(1)} %fusion.8) | data formatting | bytes 6291456
  83.2 12.6 %convolution_convert_fusion = bf16[512,3072]{1,0:T(8,128)(2,1)} fusion(bf16[2048,3072]{1,0:T(8,128)(2,1)} %param.8, bf16[2048,512]{1,0:T(8,128)(2,1)} %param.10, bf16[2048,512]{1,0:T(8,128)(2,1)} %param.9), kind=kOutput, calls=%fused_computation.7 | convolution fusion | flops 6452412416 | bytes 19922944 | tf_op jit(solution)/shard_map/dot_general | solution.py:20
  95.8 106.1 %all-reduce.2.cloned.1.call-done = bf16[2048,3072]{1,0:T(8,128)(2,1)} async-done(((bf16[2048,3072]{1,0:T(8,128)(2,1)}), bf16[2048,3072]{1,0:T(8,128)(2,1)}) %all-reduce.2.cloned.1.call-update) | async-done | bytes 12582928 | tf_op jit(solution)/shard_map/psum | solution.py:17
  201.9 0.0 copy-start.1
  201.9 10.8 %copy.14 = bf16[2048,3072]{1,0:T(8,128)(2,1)} copy(bf16[2048,3072]{1,0:T(8,128)(2,1)} %all-reduce.2.cloned.1.call-done) | data formatting | bytes 25165824
  212.7 0.0 copy-done.1
Async XLA Ops:
  7.2 16.1 %copy-start = (bf16[3072,512]{1,0:T(8,128)(2,1)S(1)}, bf16[3072,512]{1,0:T(8,128)(2,1)}, u32[]{:S(2)}) copy-start(bf16[3072,512]{1,0:T(8,128)(2,1)} %param.11) | copy-start | bytes 9437188
  7.2 194.7 %all-reduce.2.cloned.1.call-start = ((), (), s32[]{:S(2)}) async-start(), calls=%async_computation | async-start | bytes 25165824 | tf_op jit(solution)/shard_map/psum | solution.py:17
  23.3 12.0 %copy-start.4 = (bf16[2048,512]{1,0:T(8,128)(2,1)}, bf16[2048,512]{1,0:T(8,128)(2,1)S(1)}, u32[]{:S(2)}) copy-start(bf16[2048,512]{1,0:T(8,128)(2,1)S(1)} %get-tuple-element.8) | copy-start | bytes 6291460
  23.3 12.0 %copy-start.2 = (bf16[3072,512]{1,0:T(8,128)(2,1)S(1)}, bf16[3072,512]{1,0:T(8,128)(2,1)}, u32[]{:S(2)}) copy-start(bf16[3072,512]{1,0:T(8,128)(2,1)} %param.12) | copy-start | bytes 9437188
  23.3 12.0 %copy-start.3 = (bf16[2048,512]{1,0:T(8,128)(2,1)S(1)}, bf16[2048,512]{1,0:T(8,128)(2,1)}, u32[]{:S(2)}) copy-start(bf16[2048,512]{1,0:T(8,128)(2,1)} %param.9) | copy-start | bytes 6291460
  201.9 10.8 %copy-start.1 = (bf16[3072,512]{1,0:T(8,128)(2,1)S(1)}, bf16[3072,512]{1,0:T(8,128)(2,1)}, u32[]{:S(2)}) copy-start(bf16[3072,512]{1,0:T(8,128)(2,1)} %param.11) | copy-start | bytes 9437188
Sparse Core Ops, SparseCore 0:
  54.1 147.6 all-reduce.1
where the time goes:
time: 220 us
  waiting for transfers between devices  106 us (48%)
  matrix products  82.9 us (38%)
  local copies, waits for them, and re-layouts  16.4 us (7%)
  between operations  14.1 us (6%)
    psum x1, waiting for transfers between devices, step(): dx = lax.psum(term.astype(jnp.bfloat16), 'tp')  106 us
    dot_general x1, matrix products, step(): jnp.dot(d_up, w_up.T, preferred_element_type=jnp.float32)  18.7 us
    unnamed x13, local copies, waits for them, and re-layouts  16.4 us
    dot_general x1, matrix products, step(): d_hidden = jnp.dot(dy, w_down.T, preferred_element_type=jnp.float32)  16.1 us
    dot_general x1, matrix products, step(): dw_up = jnp.dot(x.T, d_up, preferred_element_type=jnp.float32)  13 us
    dot_general x1, matrix products, step(): jnp.dot(hidden.astype(jnp.bfloat16).T, dy, preferred_element_type=jnp.flo...  12.6 us
    dot_general x1, matrix products, step(): jnp.dot(d_gate, w_gate.T, preferred_element_type=jnp.float32)  12 us
    dot_general x1, matrix products, step(): dw_gate = jnp.dot(x.T, d_gate, preferred_element_type=jnp.float32)  10.6 us
  transfers between devices with their start and end apart: 1, of which 1 were waited for; matrix products, arithmetic and copies ran while one was open for 19% of the time, Pallas kernels for 0%

commit v1 on v0

v1 whole, which is shorter than its diff:
```python
import functools

import jax
import jax.numpy as jnp
from jax import lax
from jax.experimental import pallas as pl
from jax.experimental.pallas import tpu as pltpu
from jax.sharding import PartitionSpec as P

MESH = pl.DeviceIdType.MESH
CHUNKS = 8
TILE = 256
ORDERS = ((8, 4, 2), (4, 2, 8), (2, 8, 4))


def dot_nt(a, b):
    return lax.dot_general(a, b, (((1,), (1,)), ((), ())), preferred_element_type=jnp.float32)


def dot_tn(a, b):
    return lax.dot_general(a, b, (((0,), (0,)), ((), ())), preferred_element_type=jnp.float32)


def kernel(
    x, dy, gate, up, wg, wu, wdn, dx, dwg, dwu, dwd,
    wgu, wd, dyb, gb, ub, d, hid_t, own, s0, s1, s2, s3, r0, r1, r2, r3, xb, yb, og, od,
    w_sem, in_sem, xy_sem, out_sem, s_sems, r_sems, ag_send, fwd_send, fwd_recv,
):
    rows, width = dx.shape
    ff = gate.shape[1]
    R = rows // CHUNKS
    C = width // 6
    dp = lax.axis_index("dp")
    me = lax.axis_index("tp")
    core = lax.rem(me, 2)
    mate = me + 1 - 2 * core
    bits = {s: lax.rem(me // s, 2) for s in (2, 4, 8)}
    peer = {s: me + (1 - 2 * bits[s]) * s for s in (2, 4, 8)}
    units = width // TILE

    def fetch(t):
        sl = lax.rem(t, 2)
        r = pl.ds(t * R, R)
        return (
            pltpu.make_async_copy(dy.at[r, :], dyb.at[sl], in_sem.at[0, sl]),
            pltpu.make_async_copy(gate.at[r, :], gb.at[sl], in_sem.at[1, sl]),
            pltpu.make_async_copy(up.at[r, :], ub.at[sl], in_sem.at[2, sl]),
        )

    def fetch_cols(u):
        sl = lax.rem(u, 2)
        c = pl.ds(pl.multiple_of(u * TILE, TILE), TILE)
        return (
            pltpu.make_async_copy(x.at[:, c], xb.at[sl], xy_sem.at[0, sl]),
            pltpu.make_async_copy(dy.at[:, c], yb.at[sl], xy_sem.at[1, sl]),
        )

    def put(u):
        sl = lax.rem(u, 2)
        c = pl.ds(pl.multiple_of(u * TILE, TILE), TILE)
        return (
            pltpu.make_async_copy(og.at[sl, :, pl.ds(0, ff)], dwg.at[c, :], out_sem.at[0, sl]),
            pltpu.make_async_copy(og.at[sl, :, pl.ds(ff, ff)], dwu.at[c, :], out_sem.at[1, sl]),
            pltpu.make_async_copy(od.at[sl], dwd.at[:, c], out_sem.at[2, sl]),
        )

    weights = (
        pltpu.make_async_copy(wdn, wd, w_sem.at[0]),
        pltpu.make_async_copy(wg, wgu.at[:, pl.ds(0, ff)], w_sem.at[1]),
        pltpu.make_async_copy(wu, wgu.at[:, pl.ds(ff, ff)], w_sem.at[2]),
    )
    weights[0].start()
    for c in fetch(0):
        c.start()
    weights[1].start()
    weights[2].start()

    barrier = pltpu.get_barrier_semaphore()
    for to in (mate, peer[2], peer[4], peer[8]):
        pl.semaphore_signal(barrier, inc=1, device_id=(dp, to), device_id_type=MESH)
    pl.semaphore_wait(barrier, 4)
    weights[0].wait()

    def halves(p):
        n, kept, out = R, 0, []
        for s in ORDERS[p]:
            n //= 2
            out.append((n, kept + bits[s] * n, kept + (1 - bits[s]) * n, s))
            kept = kept + bits[s] * n
        return out

    def remote(src, dst, send, recv, to):
        return pltpu.make_async_remote_copy(
            src_ref=src, dst_ref=dst, send_sem=send, recv_sem=recv, device_id=(dp, to), device_id_type=MESH
        )

    sends, recvs = (s0, s1, s2, s3), (r0, r1, r2, r3)

    def reduce_copy(stage, k, p):
        sl = lax.rem(k, 2)
        to = mate if stage == 0 else peer[ORDERS[p][stage - 1]]
        return remote(
            sends[stage].at[sl, p], recvs[stage].at[k, p], s_sems.at[stage, sl, p], r_sems.at[stage, k, p], to
        )

    def out_slice(k, p, off, n, c):
        row = pl.multiple_of(k * R + off, n)
        col = pl.multiple_of(p * 2 * C + c * C, C)
        return dx.at[pl.ds(row, n), pl.ds(col, C)]

    def gather_copy(stage, k, p):
        n, kept, _, s = halves(p)[2 - stage]
        ref = out_slice(k, p, kept, n, core)
        return remote(ref, ref, ag_send, r_sems.at[4 + stage, k, p], peer[s])

    def forward_copy(k, p, off, n):
        ref = out_slice(k, p, off, n, core)
        return remote(ref, ref, fwd_send, fwd_recv, mate)

    def partial(k, p, stage, off, n):
        hs = halves(p)
        sl = lax.rem(k, 4)
        total = own[sl, p, pl.ds(pl.multiple_of(off, n), n), :]
        base = 0
        for i in range(stage):
            total += recvs[i][k, p, pl.ds(pl.multiple_of(off - base, n), n), :].astype(jnp.float32)
            base = hs[i][1] if i < 3 else base
        return total

    def reduce_step(stage, k):
        sl = lax.rem(k, 2)

        @pl.when(k >= 2)
        def _():
            for p in range(3):
                reduce_copy(stage, k - 2, p).wait_send()

        for p in range(3):
            n, _, sent, _ = halves(p)[stage - 1]
            reduce_copy(stage - 1, k, p).wait_recv()
            sends[stage][sl, p] = partial(k, p, stage, sent, n).astype(jnp.bfloat16)
            reduce_copy(stage, k, p).start()

    def finish_step(k):
        for p in range(3):
            n, kept, _, _ = halves(p)[2]
            reduce_copy(3, k, p).wait_recv()
            row = pl.multiple_of(k * R + kept, n)
            col = pl.multiple_of(p * 2 * C + core * C, C)
            dx[pl.ds(row, n), pl.ds(col, C)] = partial(k, p, 4, kept, n).astype(jnp.bfloat16)
            gather_copy(0, k, p).start()
            forward_copy(k, p, kept, n).start()

    def gather_step(stage, k):
        for p in range(3):
            n, _, other, _ = halves(p)[3 - stage]
            gather_copy(stage - 1, k, p).wait_recv()
            if stage < 3:
                gather_copy(stage, k, p).start()
            forward_copy(k, p, other, n).start()

    def live(t, lag, f):
        k = t - lag

        @pl.when((k >= 0) & (k < CHUNKS))
        def _():
            f(k)

    def hidden_grads(t):
        sl = lax.rem(t, 2)
        for c in fetch(t):
            c.wait()
        r = pl.ds(pl.multiple_of(t * R, R), R)
        step = ff // 2
        for h in range(2):
            c = pl.ds(h * step, step)
            dh = dot_nt(dyb[sl], wd[c, :])
            g = gb[sl, :, c].astype(jnp.float32)
            u = ub[sl, :, c].astype(jnp.float32)
            sg = jax.nn.sigmoid(g)
            silu = g * sg
            d[r, pl.ds(ff + h * step, step)] = (dh * silu).astype(jnp.bfloat16)
            d[r, c] = ((dh * u) * (sg * (1.0 + g * (1.0 - sg)))).astype(jnp.bfloat16)
            hid_t[c, r] = (silu * u).astype(jnp.bfloat16).T

        @pl.when(t + 1 < CHUNKS)
        def _():
            for c in fetch(t + 1):
                c.start()

    def terms(t):
        sl = lax.rem(t, 2)
        r = pl.ds(pl.multiple_of(t * R, R), R)

        @pl.when(t >= 2)
        def _():
            for p in range(3):
                reduce_copy(0, t - 2, p).wait_send()

        for p in range(3):
            w = pl.ds(pl.multiple_of(p * 2 * C + (1 - core) * C, C), C)
            s0[sl, p] = dot_nt(d[r, :], wgu[w, :]).astype(jnp.bfloat16)
            reduce_copy(0, t, p).start()
        for p in range(3):
            w = pl.ds(pl.multiple_of(p * 2 * C + core * C, C), C)
            own[lax.rem(t, 4), p] = dot_nt(d[r, :], wgu[w, :])

    def weight_grads(u):
        sl = lax.rem(u, 2)

        @pl.when(u >= 2)
        def _():
            for c in put(u - 2):
                c.wait()

        for c in fetch_cols(u):
            c.wait()
        og[sl] = dot_tn(xb[sl], d[...]).astype(jnp.bfloat16)
        od[sl] = jnp.dot(hid_t[...], yb[sl], preferred_element_type=jnp.float32).astype(jnp.bfloat16)
        for c in put(u):
            c.start()

        @pl.when(u + 2 < units)
        def _():
            for c in fetch_cols(u + 2):
                c.start()

    def step(t, _):
        @pl.when(t < CHUNKS)
        def _():
            hidden_grads(t)

        @pl.when(t == 0)
        def _():
            weights[1].wait()
            weights[2].wait()
            for u in range(2):
                for c in fetch_cols(u):
                    c.start()

        @pl.when((t >= CHUNKS) & (2 * (t - CHUNKS) < units))
        def _():
            weight_grads(2 * (t - CHUNKS))

        live(t, 1, lambda k: reduce_step(1, k))
        live(t, 2, lambda k: reduce_step(2, k))
        live(t, 3, lambda k: reduce_step(3, k))
        live(t, 4, finish_step)

        @pl.when(t < CHUNKS)
        def _():
            terms(t)

        live(t, 5, lambda k: gather_step(1, k))
        live(t, 6, lambda k: gather_step(2, k))
        live(t, 7, lambda k: gather_step(3, k))

        @pl.when((t >= CHUNKS) & (2 * (t - CHUNKS) < units))
        def _():
            weight_grads(2 * (t - CHUNKS) + 1)

        return 0

    lax.fori_loop(0, CHUNKS + 7, step, 0)

    for u in (units - 2, units - 1):
        for c in put(u):
            c.wait()
    for stage in range(4):
        for k in (CHUNKS - 2, CHUNKS - 1):
            for p in range(3):
                reduce_copy(stage, k, p).wait_send()
    part = dx.at[pl.ds(0, rows // 8 * 7), pl.ds(0, width // 2)]
    remote(part, part, ag_send, fwd_recv, mate).wait_send()
    half = dx.at[:, pl.ds(0, width // 2)]
    remote(half, half, fwd_send, fwd_recv, mate).wait()


def solution(mesh):
    def step(x, dy, gate, up, w_gate, w_up, w_down):
        rows, width = dy.shape
        ff = gate.shape[1]
        R, C, K = rows // CHUNKS, width // 6, CHUNKS
        bf, f32 = jnp.bfloat16, jnp.float32
        V, D = pltpu.VMEM, pltpu.SemaphoreType.DMA
        flops = 2 * rows * width * ff * 6
        hbm = pl.BlockSpec(memory_space=pl.ANY)
        return pl.pallas_call(
            kernel,
            out_shape=(
                jax.ShapeDtypeStruct((rows, width), bf),
                jax.ShapeDtypeStruct((width, ff), bf),
                jax.ShapeDtypeStruct((width, ff), bf),
                jax.ShapeDtypeStruct((ff, width), bf),
            ),
            in_specs=[hbm] * 7,
            out_specs=(pl.BlockSpec(memory_space=pltpu.VMEM), hbm, hbm, hbm),
            scratch_shapes=[
                V((width, 2 * ff), bf), V((ff, width), bf),
                V((2, R, width), bf), V((2, R, ff), bf), V((2, R, ff), bf),
                V((rows, 2 * ff), bf), V((ff, rows), bf),
                V((4, 3, R, C), f32),
                V((2, 3, R, C), bf), V((2, 3, R // 2, C), bf), V((2, 3, R // 4, C), bf), V((2, 3, R // 8, C), bf),
                V((K, 3, R, C), bf), V((K, 3, R // 2, C), bf), V((K, 3, R // 4, C), bf), V((K, 3, R // 8, C), bf),
                V((2, rows, TILE), bf), V((2, rows, TILE), bf),
                V((2, TILE, 2 * ff), bf), V((2, ff, TILE), bf),
                D((3,)), D((3, 2)), D((2, 2)), D((3, 2)), D((4, 2, 3)), D((7, K, 3)), D, D, D,
            ],
            compiler_params=pltpu.CompilerParams(
                collective_id=0, has_side_effects=True, vmem_limit_bytes=67_043_328
            ),
            cost_estimate=pl.CostEstimate(flops=flops, bytes_accessed=60_000_000, transcendentals=rows * ff),
            name="mlp_grads",
        )(x, dy, gate, up, w_gate, w_up, w_down)

    tokens, columns, rows = P("dp", None), P(None, "tp"), P("tp", None)
    return jax.shard_map(
        step,
        mesh=mesh,
        in_specs=(tokens, tokens, P("dp", "tp"), P("dp", "tp"), columns, columns, rows),
        out_specs=(tokens, P("dp", "tp"), P("dp", "tp"), P(("dp", "tp"), None)),
        check_vma=False,
    )
```

time: 220 us -> 122 us (0.55)
  waiting for transfers between devices: 106 us -> 0 us
  Pallas kernels: 0 us -> 102 us
  matrix products: 82.9 us -> 0 us
  between operations: 14.1 us -> 0.65 us
    psum x1 -> x0, waiting for transfers between devices: 106 us -> none  [step(): dx = lax.psum(term.astype(jnp.bfloat16), 'tp')]
    pallas_call x0 -> x1, Pallas kernels: none -> 102 us  [step(): pl.pallas_call(kernel, out_shape=(jax.ShapeDtypeStruct((rows, width), bf)...]
    dot_general x6 -> x0, matrix products: 82.9 us -> none  [the longest x1 18.7 us: step(): jnp.dot(d_up, w_up.T, preferred_element_type=jnp.float32)]
    unnamed x13 -> x10, local copies, waits for them, and re-layouts: 16.4 us -> 18.5 us
  transfers between devices with their start and end apart: 1 -> 0, of which waited for: 1 -> 0; matrix products, arithmetic and copies ran while one was open for 19% -> 0% of each run, Pallas kernels for 0% -> 0%
where the time goes in v1:
time: 122 us; the launch traced here: 121 us
  Pallas kernels  102 us (84%)
  local copies, waits for them, and re-layouts  18.5 us (15%)
    pallas_call x1, Pallas kernels, step(): pl.pallas_call(kernel, out_shape=(jax.ShapeDtypeStruct((rows, width), bf)...  102 us
    unnamed x10, local copies, waits for them, and re-layouts  18.5 us

profile of v1, /device:TPU:0, one launch (start us, length us, event | category | flops | bytes accessed | tf_op | source)
XLA Modules:
  0.0 121.4 jit_solution(7491612317750540951)
XLA Ops:
  0.6 102.2 %mlp_grads.1 = (bf16[2048,3072]{1,0:T(8,128)(2,1)}, bf16[3072,512]{1,0:T(8,128)(2,1)}, bf16[3072,512]{1,0:T(8,128)(2,1)}, bf16[512,3072]{1,0:T(8,128)(2,1)}) custom-call(bf16[2048,3072]{1,0:T(8,128)(2,1)} %x.1, bf16[2048,3072]{1,0:T(8,128)(2,1)} %dy.1, bf16[2048,512]{1,0:T(8,128)(2,1)} %gate.1, bf16[2048,512]{1,0:T(8,128)(2,1)} %up.1, bf16[3072,512]{1,0:T(8,128)(2,1)} %wg.1, ...), custom_call_target="tpu_custom_call" | custom-call | flops 38654705664 | bytes 60000000 | tf_op jit(solution)/shard_map/mlp_grads/pallas_call | solution.py:288
  102.8 0.0 copy-start.2
  102.8 10.8 %copy.15 = bf16[2048,3072]{1,0:T(8,128)(2,1)} copy(bf16[2048,3072]{1,0:T(8,128)(2,1)} %get-tuple-element.8) | data formatting | bytes 25165824
  113.7 0.0 copy-done.2
  113.7 0.0 copy-start.1
  113.7 1.7 %copy.16 = bf16[3072,512]{1,0:T(8,128)(2,1)} copy(bf16[3072,512]{1,0:T(8,128)(2,1)S(1)} %copy-done.2) | data formatting | bytes 6291456
  115.3 1.4 %copy-done.1 = bf16[3072,512]{1,0:T(8,128)(2,1)S(1)} copy-done((bf16[3072,512]{1,0:T(8,128)(2,1)S(1)}, bf16[3072,512]{1,0:T(8,128)(2,1)}, u32[]{:S(2)}) %copy-start.1) | copy-done | bytes 3145752
  116.7 0.0 copy-start
  116.7 1.7 %copy.17 = bf16[3072,512]{1,0:T(8,128)(2,1)} copy(bf16[3072,512]{1,0:T(8,128)(2,1)S(1)} %copy-done.1) | data formatting | bytes 6291456
  118.4 1.4 %copy-done = bf16[512,3072]{1,0:T(8,128)(2,1)S(1)} copy-done((bf16[512,3072]{1,0:T(8,128)(2,1)S(1)}, bf16[512,3072]{1,0:T(8,128)(2,1)}, u32[]{:S(2)}) %copy-start) | copy-done | bytes 3145752
  119.7 1.7 %copy.18 = bf16[512,3072]{1,0:T(8,128)(2,1)} copy(bf16[512,3072]{1,0:T(8,128)(2,1)S(1)} %copy-done) | data formatting | bytes 6291456
Async XLA Ops:
  102.8 10.8 %copy-start.2 = (bf16[3072,512]{1,0:T(8,128)(2,1)S(1)}, bf16[3072,512]{1,0:T(8,128)(2,1)}, u32[]{:S(2)}) copy-start(bf16[3072,512]{1,0:T(8,128)(2,1)} %get-tuple-element.9) | copy-start | bytes 9437188
  113.7 3.0 %copy-start.1 = (bf16[3072,512]{1,0:T(8,128)(2,1)S(1)}, bf16[3072,512]{1,0:T(8,128)(2,1)}, u32[]{:S(2)}) copy-start(bf16[3072,512]{1,0:T(8,128)(2,1)} %get-tuple-element.10) | copy-start | bytes 9437188
  116.7 3.0 %copy-start = (bf16[512,3072]{1,0:T(8,128)(2,1)S(1)}, bf16[512,3072]{1,0:T(8,128)(2,1)}, u32[]{:S(2)}) copy-start(bf16[512,3072]{1,0:T(8,128)(2,1)} %get-tuple-element.11) | copy-start | bytes 9437188

commit v2 on v1

--- a/solution.py
+++ b/solution.py
@@ -23,10 +23,10 @@
 
 def kernel(
     x, dy, gate, up, wg, wu, wdn, dx, dwg, dwu, dwd,
-    wgu, wd, dyb, gb, ub, d, hid_t, own, s0, s1, s2, s3, r0, r1, r2, r3, xb, yb, og, od,
-    w_sem, in_sem, xy_sem, out_sem, s_sems, r_sems, ag_send, fwd_send, fwd_recv,
+    dyb, gb, ub, d, hid_t, own, s0, s1, s2, s3, r0, r1, r2, r3, xb, yb,
+    w_sem, in_sem, xy_sem, s_sems, r_sems, ag_send, fwd_send, fwd_recv,
 ):
-    rows, width = dx.shape
+    rows, width = dy.shape
     ff = gate.shape[1]
     R = rows // CHUNKS
     C = width // 6
@@ -55,19 +55,10 @@
             pltpu.make_async_copy(dy.at[:, c], yb.at[sl], xy_sem.at[1, sl]),
         )
 
-    def put(u):
-        sl = lax.rem(u, 2)
-        c = pl.ds(pl.multiple_of(u * TILE, TILE), TILE)
-        return (
-            pltpu.make_async_copy(og.at[sl, :, pl.ds(0, ff)], dwg.at[c, :], out_sem.at[0, sl]),
-            pltpu.make_async_copy(og.at[sl, :, pl.ds(ff, ff)], dwu.at[c, :], out_sem.at[1, sl]),
-            pltpu.make_async_copy(od.at[sl], dwd.at[:, c], out_sem.at[2, sl]),
-        )
-
     weights = (
-        pltpu.make_async_copy(wdn, wd, w_sem.at[0]),
-        pltpu.make_async_copy(wg, wgu.at[:, pl.ds(0, ff)], w_sem.at[1]),
-        pltpu.make_async_copy(wu, wgu.at[:, pl.ds(ff, ff)], w_sem.at[2]),
+        pltpu.make_async_copy(wdn, dwd, w_sem.at[0]),
+        pltpu.make_async_copy(wg, dwg, w_sem.at[1]),
+        pltpu.make_async_copy(wu, dwu, w_sem.at[2]),
     )
     weights[0].start()
     for c in fetch(0):
@@ -105,8 +96,7 @@
 
     def out_slice(k, p, off, n, c):
         row = pl.multiple_of(k * R + off, n)
-        col = pl.multiple_of(p * 2 * C + c * C, C)
-        return dx.at[pl.ds(row, n), pl.ds(col, C)]
+        return dx.at[2 * p + c, pl.ds(row, n), :]
 
     def gather_copy(stage, k, p):
         n, kept, _, s = halves(p)[2 - stage]
@@ -146,8 +136,7 @@
             n, kept, _, _ = halves(p)[2]
             reduce_copy(3, k, p).wait_recv()
             row = pl.multiple_of(k * R + kept, n)
-            col = pl.multiple_of(p * 2 * C + core * C, C)
-            dx[pl.ds(row, n), pl.ds(col, C)] = partial(k, p, 4, kept, n).astype(jnp.bfloat16)
+            dx[2 * p + core, pl.ds(row, n), :] = partial(k, p, 4, kept, n).astype(jnp.bfloat16)
             gather_copy(0, k, p).start()
             forward_copy(k, p, kept, n).start()
 
@@ -174,7 +163,7 @@
         step = ff // 2
         for h in range(2):
             c = pl.ds(h * step, step)
-            dh = dot_nt(dyb[sl], wd[c, :])
+            dh = dot_nt(dyb[sl], dwd[c, :])
             g = gb[sl, :, c].astype(jnp.float32)
             u = ub[sl, :, c].astype(jnp.float32)
             sg = jax.nn.sigmoid(g)
@@ -188,6 +177,9 @@
             for c in fetch(t + 1):
                 c.start()
 
+    def term(r, w):
+        return dot_nt(d[r, pl.ds(0, ff)], dwg[w, :]) + dot_nt(d[r, pl.ds(ff, ff)], dwu[w, :])
+
     def terms(t):
         sl = lax.rem(t, 2)
         r = pl.ds(pl.multiple_of(t * R, R), R)
@@ -199,26 +191,21 @@
 
         for p in range(3):
             w = pl.ds(pl.multiple_of(p * 2 * C + (1 - core) * C, C), C)
-            s0[sl, p] = dot_nt(d[r, :], wgu[w, :]).astype(jnp.bfloat16)
+            s0[sl, p] = term(r, w).astype(jnp.bfloat16)
             reduce_copy(0, t, p).start()
         for p in range(3):
             w = pl.ds(pl.multiple_of(p * 2 * C + core * C, C), C)
-            own[lax.rem(t, 4), p] = dot_nt(d[r, :], wgu[w, :])
+            own[lax.rem(t, 4), p] = term(r, w)
 
     def weight_grads(u):
         sl = lax.rem(u, 2)
 
-        @pl.when(u >= 2)
-        def _():
-            for c in put(u - 2):
-                c.wait()
-
         for c in fetch_cols(u):
             c.wait()
-        og[sl] = dot_tn(xb[sl], d[...]).astype(jnp.bfloat16)
-        od[sl] = jnp.dot(hid_t[...], yb[sl], preferred_element_type=jnp.float32).astype(jnp.bfloat16)
-        for c in put(u):
-            c.start()
+        c = pl.ds(pl.multiple_of(u * TILE, TILE), TILE)
+        dwg[c, :] = dot_tn(xb[sl], d[:, pl.ds(0, ff)]).astype(jnp.bfloat16)
+        dwu[c, :] = dot_tn(xb[sl], d[:, pl.ds(ff, ff)]).astype(jnp.bfloat16)
+        dwd[:, c] = jnp.dot(hid_t[...], yb[sl], preferred_element_type=jnp.float32).astype(jnp.bfloat16)
 
         @pl.when(u + 2 < units)
         def _():
@@ -263,17 +250,24 @@
 
     lax.fori_loop(0, CHUNKS + 7, step, 0)
 
-    for u in (units - 2, units - 1):
-        for c in put(u):
-            c.wait()
     for stage in range(4):
         for k in (CHUNKS - 2, CHUNKS - 1):
             for p in range(3):
                 reduce_copy(stage, k, p).wait_send()
-    part = dx.at[pl.ds(0, rows // 8 * 7), pl.ds(0, width // 2)]
+    part = dx.at[pl.ds(0, 3), pl.ds(0, rows // 8 * 7), :]
     remote(part, part, ag_send, fwd_recv, mate).wait_send()
-    half = dx.at[:, pl.ds(0, width // 2)]
+    half = dx.at[pl.ds(0, 3)]
     remote(half, half, fwd_send, fwd_recv, mate).wait()
+
+
+def write_out(a, g, u, e, dx, dwg, dwu, dwd, sem):
+    C = a.shape[2]
+    copies = [pltpu.make_async_copy(a.at[j], dx.at[:, pl.ds(j * C, C)], sem.at[j]) for j in range(6)]
+    copies += [pltpu.make_async_copy(s, t, sem.at[6 + j]) for j, (s, t) in enumerate(((g, dwg), (u, dwu), (e, dwd)))]
+    for c in copies:
+        c.start()
+    for c in copies:
+        c.wait()
 
 
 def solution(mesh):
@@ -284,34 +278,41 @@
         bf, f32 = jnp.bfloat16, jnp.float32
         V, D = pltpu.VMEM, pltpu.SemaphoreType.DMA
         flops = 2 * rows * width * ff * 6
-        hbm = pl.BlockSpec(memory_space=pl.ANY)
+        hbm, vmem = pl.BlockSpec(memory_space=pl.ANY), pl.BlockSpec(memory_space=pltpu.VMEM)
+        grads = pl.pallas_call(
+            kernel,
+            out_shape=(V((6, rows, C), bf), V((width, ff), bf), V((width, ff), bf), V((ff, width), bf)),
+            in_specs=[hbm] * 7,
+            out_specs=[vmem] * 4,
+            scratch_shapes=[
+                V((2, R, width), bf), V((2, R, ff), bf), V((2, R, ff), bf),
+                V((rows, 2 * ff), bf), V((ff, rows), bf),
+                V((4, 3, R, C), f32),
+                V((2, 3, R, C), bf), V((2, 3, R // 2, C), bf), V((2, 3, R // 4, C), bf), V((2, 3, R // 8, C), bf),
+                V((K, 3, R, C), bf), V((K, 3, R // 2, C), bf), V((K, 3, R // 4, C), bf), V((K, 3, R // 8, C), bf),
+                V((2, rows, TILE), bf), V((2, rows, TILE), bf),
+                D((3,)), D((3, 2)), D((2, 2)), D((4, 2, 3)), D((7, K, 3)), D, D, D,
+            ],
+            compiler_params=pltpu.CompilerParams(
+                collective_id=0, has_side_effects=True, vmem_limit_bytes=44_000_000
+            ),
+            cost_estimate=pl.CostEstimate(flops=flops, bytes_accessed=60_000_000, transcendentals=rows * ff),
+            name="mlp_grads",
+        )(x, dy, gate, up, w_gate, w_up, w_down)
         return pl.pallas_call(
-            kernel,
+            write_out,
             out_shape=(
                 jax.ShapeDtypeStruct((rows, width), bf),
                 jax.ShapeDtypeStruct((width, ff), bf),
                 jax.ShapeDtypeStruct((width, ff), bf),
                 jax.ShapeDtypeStruct((ff, width), bf),
             ),
-            in_specs=[hbm] * 7,
-            out_specs=(pl.BlockSpec(memory_space=pltpu.VMEM), hbm, hbm, hbm),
-            scratch_shapes=[
-                V((width, 2 * ff), bf), V((ff, width), bf),
-                V((2, R, width), bf), V((2, R, ff), bf), V((2, R, ff), bf),
-                V((rows, 2 * ff), bf), V((ff, rows), bf),
-                V((4, 3, R, C), f32),
-                V((2, 3, R, C), bf), V((2, 3, R // 2, C), bf), V((2, 3, R // 4, C), bf), V((2, 3, R // 8, C), bf),
-                V((K, 3, R, C), bf), V((K, 3, R // 2, C), bf), V((K, 3, R // 4, C), bf), V((K, 3, R // 8, C), bf),
-                V((2, rows, TILE), bf), V((2, rows, TILE), bf),
-                V((2, TILE, 2 * ff), bf), V((2, ff, TILE), bf),
-                D((3,)), D((3, 2)), D((2, 2)), D((3, 2)), D((4, 2, 3)), D((7, K, 3)), D, D, D,
-            ],
-            compiler_params=pltpu.CompilerParams(
-                collective_id=0, has_side_effects=True, vmem_limit_bytes=67_043_328
-            ),
-            cost_estimate=pl.CostEstimate(flops=flops, bytes_accessed=60_000_000, transcendentals=rows * ff),
-            name="mlp_grads",
-        )(x, dy, gate, up, w_gate, w_up, w_down)
+            in_specs=[vmem] * 4,
+            out_specs=[hbm] * 4,
+            scratch_shapes=[D((9,))],
+            compiler_params=pltpu.CompilerParams(vmem_limit_bytes=1_000_000),
+            name="write_out",
+        )(*grads)
 
     tokens, columns, rows = P("dp", None), P(None, "tp"), P("tp", None)
     return jax.shard_map(

time: 122 us -> 106 us (0.87)
  local copies, waits for them, and re-layouts: 18.5 us -> 0 us
  Pallas kernels: 102 us -> 105 us
    unnamed x10 -> x0, local copies, waits for them, and re-layouts: 18.5 us -> none
    pallas_call x1 -> x2, Pallas kernels: 102 us -> 105 us  [the longest x1 97.6 us: step(): pl.pallas_call(kernel, out_shape=(V((6, rows, C), bf), V((width, ff), bf)...]
where the time goes in v2:
time: 106 us
  Pallas kernels  105 us (99%)
    pallas_call x1, Pallas kernels, step(): pl.pallas_call(kernel, out_shape=(V((6, rows, C), bf), V((width, ff), bf)...  97.6 us
    pallas_call x1, Pallas kernels, step(): pl.pallas_call(write_out, out_shape=(jax.ShapeDtypeStruct((rows, width),...  7.54 us

profile of v2, /device:TPU:0, one launch (start us, length us, event | category | flops | bytes accessed | tf_op | source)
XLA Modules:
  0.0 105.8 jit_solution(2273397532220163275)
XLA Ops:
  0.6 97.6 %mlp_grads.1 = (bf16[6,2048,512]{2,1,0:T(8,128)(2,1)S(1)}, bf16[3072,512]{1,0:T(8,128)(2,1)S(1)}, bf16[3072,512]{1,0:T(8,128)(2,1)S(1)}, bf16[512,3072]{1,0:T(8,128)(2,1)S(1)}) custom-call(bf16[2048,3072]{1,0:T(8,128)(2,1)} %x.1, bf16[2048,3072]{1,0:T(8,128)(2,1)} %dy.1, bf16[2048,512]{1,0:T(8,128)(2,1)} %gate.1, bf16[2048,512]{1,0:T(8,128)(2,1)} %up.1, ...), custom_call_target="tpu_custom_call" | custom-call | flops 38654705664 | bytes 60000000 | tf_op jit(solution)/shard_map/mlp_grads/pallas_call | solution.py:282
  98.2 7.5 %write_out.1 = (bf16[2048,3072]{1,0:T(8,128)(2,1)}, bf16[3072,512]{1,0:T(8,128)(2,1)}, bf16[3072,512]{1,0:T(8,128)(2,1)}, bf16[512,3072]{1,0:T(8,128)(2,1)}) custom-call(bf16[6,2048,512]{2,1,0:T(8,128)(2,1)S(1)} %get-tuple-element.8.a, bf16[3072,512]{1,0:T(8,128)(2,1)S(1)} %get-tuple-element.9.g, bf16[3072,512]{1,0:T(8,128)(2,1)S(1)} %get-tuple-element.10.u, ...), custom_call_target="tpu_custom_call" | custom-call | tf_op jit(solution)/shard_map/write_out/pallas_call | solution.py:302

commit v3 on v2

--- a/solution.py
+++ b/solution.py
@@ -10,6 +10,8 @@
 MESH = pl.DeviceIdType.MESH
 CHUNKS = 8
 TILE = 256
+LAGS = (0, 2, 4, 6, 8, 10, 12)
+SLOTS = (2, 3, 4, 4)
 ORDERS = ((8, 4, 2), (4, 2, 8), (2, 8, 4))
 
 
@@ -55,22 +57,32 @@
             pltpu.make_async_copy(dy.at[:, c], yb.at[sl], xy_sem.at[1, sl]),
         )
 
-    weights = (
-        pltpu.make_async_copy(wdn, dwd, w_sem.at[0]),
-        pltpu.make_async_copy(wg, dwg, w_sem.at[1]),
-        pltpu.make_async_copy(wu, dwu, w_sem.at[2]),
-    )
-    weights[0].start()
+    def down_half(h):
+        r = pl.ds(h * (ff // 2), ff // 2)
+        return pltpu.make_async_copy(wdn.at[r, :], dwd.at[r, :], w_sem.at[h])
+
+    def columns_of(p, c):
+        return pl.ds(pl.multiple_of(p * 2 * C + c * C, C), C)
+
+    def weight_tile(i):
+        w = columns_of(i % 3, core if i >= 3 else 1 - core)
+        return (
+            pltpu.make_async_copy(wg.at[w, :], dwg.at[w, :], w_sem.at[2 + i]),
+            pltpu.make_async_copy(wu.at[w, :], dwu.at[w, :], w_sem.at[8 + i]),
+        )
+
+    down_half(0).start()
     for c in fetch(0):
         c.start()
-    weights[1].start()
-    weights[2].start()
+    down_half(1).start()
 
     barrier = pltpu.get_barrier_semaphore()
     for to in (mate, peer[2], peer[4], peer[8]):
         pl.semaphore_signal(barrier, inc=1, device_id=(dp, to), device_id_type=MESH)
     pl.semaphore_wait(barrier, 4)
-    weights[0].wait()
+    for i in range(6):
+        for c in weight_tile(i):
+            c.start()
 
     def halves(p):
         n, kept, out = R, 0, []
@@ -88,10 +100,14 @@
     sends, recvs = (s0, s1, s2, s3), (r0, r1, r2, r3)
 
     def reduce_copy(stage, k, p):
-        sl = lax.rem(k, 2)
+        sl = lax.rem(k, SLOTS[stage])
         to = mate if stage == 0 else peer[ORDERS[p][stage - 1]]
         return remote(
-            sends[stage].at[sl, p], recvs[stage].at[k, p], s_sems.at[stage, sl, p], r_sems.at[stage, k, p], to
+            sends[stage].at[sl, p],
+            recvs[stage].at[k, p],
+            s_sems.at[stage, sl, p],
+            r_sems.at[stage, k, p],
+            to,
         )
 
     def out_slice(k, p, off, n, c):
@@ -109,8 +125,10 @@
 
     def partial(k, p, stage, off, n):
         hs = halves(p)
-        sl = lax.rem(k, 4)
-        total = own[sl, p, pl.ds(pl.multiple_of(off, n), n), :]
+        if stage == 1:
+            total = own[CHUNKS, p]
+        else:
+            total = own[k, p, pl.ds(pl.multiple_of(off - hs[0][1], n), n), :]
         base = 0
         for i in range(stage):
             total += recvs[i][k, p, pl.ds(pl.multiple_of(off - base, n), n), :].astype(jnp.float32)
@@ -118,12 +136,15 @@
         return total
 
     def reduce_step(stage, k):
-        sl = lax.rem(k, 2)
-
-        @pl.when(k >= 2)
-        def _():
-            for p in range(3):
-                reduce_copy(stage, k - 2, p).wait_send()
+        m = SLOTS[stage]
+        sl = lax.rem(k, m)
+
+        if not isinstance(k, int):
+
+            @pl.when(k >= m)
+            def _():
+                for p in range(3):
+                    reduce_copy(stage, k - m, p).wait_send()
 
         for p in range(3):
             n, _, sent, _ = halves(p)[stage - 1]
@@ -157,6 +178,11 @@
 
     def hidden_grads(t):
         sl = lax.rem(t, 2)
+        @pl.when(t + 1 < CHUNKS)
+        def _():
+            for c in fetch(t + 1):
+                c.start()
+
         for c in fetch(t):
             c.wait()
         r = pl.ds(pl.multiple_of(t * R, R), R)
@@ -172,30 +198,38 @@
             d[r, c] = ((dh * u) * (sg * (1.0 + g * (1.0 - sg)))).astype(jnp.bfloat16)
             hid_t[c, r] = (silu * u).astype(jnp.bfloat16).T
 
-        @pl.when(t + 1 < CHUNKS)
-        def _():
-            for c in fetch(t + 1):
-                c.start()
-
     def term(r, w):
         return dot_nt(d[r, pl.ds(0, ff)], dwg[w, :]) + dot_nt(d[r, pl.ds(ff, ff)], dwu[w, :])
+
+    def await_tiles(t, first):
+        if isinstance(t, int):
+            for i in range(first, first + 3):
+                for c in weight_tile(i):
+                    c.wait()
 
     def terms(t):
         sl = lax.rem(t, 2)
         r = pl.ds(pl.multiple_of(t * R, R), R)
 
-        @pl.when(t >= 2)
-        def _():
-            for p in range(3):
-                reduce_copy(0, t - 2, p).wait_send()
-
-        for p in range(3):
-            w = pl.ds(pl.multiple_of(p * 2 * C + (1 - core) * C, C), C)
+        if not isinstance(t, int):
+
+            @pl.when(t >= 2)
+            def _():
+                for p in range(3):
+                    reduce_copy(0, t - 2, p).wait_send()
+
+        await_tiles(t, 0)
+        for p in range(3):
+            w = columns_of(p, 1 - core)
             s0[sl, p] = term(r, w).astype(jnp.bfloat16)
             reduce_copy(0, t, p).start()
-        for p in range(3):
-            w = pl.ds(pl.multiple_of(p * 2 * C + core * C, C), C)
-            own[lax.rem(t, 4), p] = term(r, w)
+        await_tiles(t, 3)
+        for p in range(3):
+            w = columns_of(p, core)
+            total = term(r, w)
+            for i in range(2):
+                kept = bits[ORDERS[p][0]] if i else 1 - bits[ORDERS[p][0]]
+                own[kept * t + (1 - kept) * CHUNKS, p] = total[i * (R // 2) : (i + 1) * (R // 2)]
 
     def weight_grads(u):
         sl = lax.rem(u, 2)
@@ -217,10 +251,8 @@
         def _():
             hidden_grads(t)
 
-        @pl.when(t == 0)
-        def _():
-            weights[1].wait()
-            weights[2].wait()
+        @pl.when(t == CHUNKS // 2)
+        def _():
             for u in range(2):
                 for c in fetch_cols(u):
                     c.start()
@@ -229,18 +261,18 @@
         def _():
             weight_grads(2 * (t - CHUNKS))
 
-        live(t, 1, lambda k: reduce_step(1, k))
-        live(t, 2, lambda k: reduce_step(2, k))
-        live(t, 3, lambda k: reduce_step(3, k))
-        live(t, 4, finish_step)
+        live(t, LAGS[1], lambda k: reduce_step(2, k))
+        live(t, LAGS[2], lambda k: reduce_step(3, k))
+        live(t, LAGS[3], finish_step)
 
         @pl.when(t < CHUNKS)
         def _():
             terms(t)
-
-        live(t, 5, lambda k: gather_step(1, k))
-        live(t, 6, lambda k: gather_step(2, k))
-        live(t, 7, lambda k: gather_step(3, k))
+            reduce_step(1, t)
+
+        live(t, LAGS[4], lambda k: gather_step(1, k))
+        live(t, LAGS[5], lambda k: gather_step(2, k))
+        live(t, LAGS[6], lambda k: gather_step(3, k))
 
         @pl.when((t >= CHUNKS) & (2 * (t - CHUNKS) < units))
         def _():
@@ -248,10 +280,15 @@
 
         return 0
 
-    lax.fori_loop(0, CHUNKS + 7, step, 0)
+    for h in range(2):
+        down_half(h).wait()
+    hidden_grads(0)
+    terms(0)
+    reduce_step(1, 0)
+    lax.fori_loop(1, CHUNKS + LAGS[6], step, 0)
 
     for stage in range(4):
-        for k in (CHUNKS - 2, CHUNKS - 1):
+        for k in range(CHUNKS - SLOTS[stage], CHUNKS):
             for p in range(3):
                 reduce_copy(stage, k, p).wait_send()
     part = dx.at[pl.ds(0, 3), pl.ds(0, rows // 8 * 7), :]
@@ -287,11 +324,11 @@
             scratch_shapes=[
                 V((2, R, width), bf), V((2, R, ff), bf), V((2, R, ff), bf),
                 V((rows, 2 * ff), bf), V((ff, rows), bf),
-                V((4, 3, R, C), f32),
-                V((2, 3, R, C), bf), V((2, 3, R // 2, C), bf), V((2, 3, R // 4, C), bf), V((2, 3, R // 8, C), bf),
-                V((K, 3, R, C), bf), V((K, 3, R // 2, C), bf), V((K, 3, R // 4, C), bf), V((K, 3, R // 8, C), bf),
+                V((K + 1, 3, R // 2, C), f32),
+                *(V((n, 3, R >> i, C), bf) for i, n in enumerate(SLOTS)),
+                *(V((K, 3, R >> i, C), bf) for i in range(4)),
                 V((2, rows, TILE), bf), V((2, rows, TILE), bf),
-                D((3,)), D((3, 2)), D((2, 2)), D((4, 2, 3)), D((7, K, 3)), D, D, D,
+                D((14,)), D((3, 2)), D((2, 2)), D((4, max(SLOTS), 3)), D((7, K, 3)), D, D, D,
             ],
             compiler_params=pltpu.CompilerParams(
                 collective_id=0, has_side_effects=True, vmem_limit_bytes=44_000_000

time: 106 us -> 102 us (0.962)
  Pallas kernels: 105 us -> 101 us
    pallas_call x1, Pallas kernels: 97.6 us -> 93.8 us  [step(): pl.pallas_call(kernel, out_shape=(V((6, rows, C), bf), V((width, ff), bf)...]
where the time goes in v3:
time: 102 us
  Pallas kernels  101 us (99%)
    pallas_call x1, Pallas kernels, step(): pl.pallas_call(kernel, out_shape=(V((6, rows, C), bf), V((width, ff), bf)...  93.8 us
    pallas_call x1, Pallas kernels, step(): pl.pallas_call(write_out, out_shape=(jax.ShapeDtypeStruct((rows, width),...  7.54 us

profile of v3, /device:TPU:0, one launch (start us, length us, event | category | flops | bytes accessed | tf_op | source)
XLA Modules:
  0.0 102.0 jit_solution(10099946673021138927)
XLA Ops:
  0.6 93.8 %mlp_grads.1 = (bf16[6,2048,512]{2,1,0:T(8,128)(2,1)S(1)}, bf16[3072,512]{1,0:T(8,128)(2,1)S(1)}, bf16[3072,512]{1,0:T(8,128)(2,1)S(1)}, bf16[512,3072]{1,0:T(8,128)(2,1)S(1)}) custom-call(bf16[2048,3072]{1,0:T(8,128)(2,1)} %x.1, bf16[2048,3072]{1,0:T(8,128)(2,1)} %dy.1, bf16[2048,512]{1,0:T(8,128)(2,1)} %gate.1, bf16[2048,512]{1,0:T(8,128)(2,1)} %up.1, ...), custom_call_target="tpu_custom_call" | custom-call | flops 38654705664 | bytes 60000000 | tf_op jit(solution)/shard_map/mlp_grads/pallas_call | solution.py:319
  94.4 7.5 %write_out.1 = (bf16[2048,3072]{1,0:T(8,128)(2,1)}, bf16[3072,512]{1,0:T(8,128)(2,1)}, bf16[3072,512]{1,0:T(8,128)(2,1)}, bf16[512,3072]{1,0:T(8,128)(2,1)}) custom-call(bf16[6,2048,512]{2,1,0:T(8,128)(2,1)S(1)} %get-tuple-element.8.a, bf16[3072,512]{1,0:T(8,128)(2,1)S(1)} %get-tuple-element.9.g, bf16[3072,512]{1,0:T(8,128)(2,1)S(1)} %get-tuple-element.10.u, ...), custom_call_target="tpu_custom_call" | custom-call | tf_op jit(solution)/shard_map/write_out/pallas_call | solution.py:339

commit v4 on v3

--- a/solution.py
+++ b/solution.py
@@ -26,7 +26,7 @@
 def kernel(
     x, dy, gate, up, wg, wu, wdn, dx, dwg, dwu, dwd,
     dyb, gb, ub, d, hid_t, own, s0, s1, s2, s3, r0, r1, r2, r3, xb, yb,
-    w_sem, in_sem, xy_sem, s_sems, r_sems, ag_send, fwd_send, fwd_recv,
+    w_sem, in_sem, xy_sem, s_sems, r_sems, last_sems, ag_send, fwd_send, fwd_recv,
 ):
     rows, width = dy.shape
     ff = gate.shape[1]
@@ -119,6 +119,12 @@
         ref = out_slice(k, p, kept, n, core)
         return remote(ref, ref, ag_send, r_sems.at[4 + stage, k, p], peer[s])
 
+    def last_copy(i, p):
+        n, kept, _, a = halves(p)[0]
+        ref = out_slice(CHUNKS - 1, p, kept + i * (n // 2), n // 2, core)
+        recv = r_sems.at[6, CHUNKS - 1, p] if i else last_sems.at[p]
+        return remote(ref, ref, ag_send, recv, peer[a])
+
     def forward_copy(k, p, off, n):
         ref = out_slice(k, p, off, n, core)
         return remote(ref, ref, fwd_send, fwd_recv, mate)
@@ -187,9 +193,10 @@
             c.wait()
         r = pl.ds(pl.multiple_of(t * R, R), R)
         step = ff // 2
+        back = dot_nt(dyb[sl], dwd[...])
         for h in range(2):
             c = pl.ds(h * step, step)
-            dh = dot_nt(dyb[sl], dwd[c, :])
+            dh = back[:, h * step : (h + 1) * step]
             g = gb[sl, :, c].astype(jnp.float32)
             u = ub[sl, :, c].astype(jnp.float32)
             sg = jax.nn.sigmoid(g)
@@ -285,7 +292,21 @@
     hidden_grads(0)
     terms(0)
     reduce_step(1, 0)
-    lax.fori_loop(1, CHUNKS + LAGS[6], step, 0)
+    end = CHUNKS - 1 + LAGS[5]
+    lax.fori_loop(1, end, step, 0)
+    for p in range(3):
+        n, _, other, _ = halves(p)[1]
+        gather_copy(1, CHUNKS - 1, p).wait_recv()
+        last_copy(0, p).start()
+        last_copy(1, p).start()
+        forward_copy(CHUNKS - 1, p, other, n).start()
+    for k in range(end - LAGS[6], CHUNKS - 1):
+        gather_step(3, k)
+    for i in range(2):
+        for p in range(3):
+            n, _, other, _ = halves(p)[0]
+            last_copy(i, p).wait_recv()
+            forward_copy(CHUNKS - 1, p, other + i * (n // 2), n // 2).start()
 
     for stage in range(4):
         for k in range(CHUNKS - SLOTS[stage], CHUNKS):
@@ -328,7 +349,7 @@
                 *(V((n, 3, R >> i, C), bf) for i, n in enumerate(SLOTS)),
                 *(V((K, 3, R >> i, C), bf) for i in range(4)),
                 V((2, rows, TILE), bf), V((2, rows, TILE), bf),
-                D((14,)), D((3, 2)), D((2, 2)), D((4, max(SLOTS), 3)), D((7, K, 3)), D, D, D,
+                D((14,)), D((3, 2)), D((2, 2)), D((4, max(SLOTS), 3)), D((7, K, 3)), D((3,)), D, D, D,
             ],
             compiler_params=pltpu.CompilerParams(
                 collective_id=0, has_side_effects=True, vmem_limit_bytes=44_000_000

time: 102 us -> 102 us (level)
  no operation moved by 1% of the time
where the time goes in v4:
time: 102 us
  Pallas kernels  101 us (99%)
    pallas_call x1, Pallas kernels, step(): pl.pallas_call(kernel, out_shape=(V((6, rows, C), bf), V((width, ff), bf)...  93.6 us
    pallas_call x1, Pallas kernels, step(): pl.pallas_call(write_out, out_shape=(jax.ShapeDtypeStruct((rows, width),...  7.54 us

profile of v4, /device:TPU:0, one launch (start us, length us, event | category | flops | bytes accessed | tf_op | source)
XLA Modules:
  0.0 101.7 jit_solution(5813511020548552481)
XLA Ops:
  0.6 93.6 %mlp_grads.1 = (bf16[6,2048,512]{2,1,0:T(8,128)(2,1)S(1)}, bf16[3072,512]{1,0:T(8,128)(2,1)S(1)}, bf16[3072,512]{1,0:T(8,128)(2,1)S(1)}, bf16[512,3072]{1,0:T(8,128)(2,1)S(1)}) custom-call(bf16[2048,3072]{1,0:T(8,128)(2,1)} %x.1, bf16[2048,3072]{1,0:T(8,128)(2,1)} %dy.1, bf16[2048,512]{1,0:T(8,128)(2,1)} %gate.1, bf16[2048,512]{1,0:T(8,128)(2,1)} %up.1, ...), custom_call_target="tpu_custom_call" | custom-call | flops 38654705664 | bytes 60000000 | tf_op jit(solution)/shard_map/mlp_grads/pallas_call | solution.py:340
  94.2 7.5 %write_out.1 = (bf16[2048,3072]{1,0:T(8,128)(2,1)}, bf16[3072,512]{1,0:T(8,128)(2,1)}, bf16[3072,512]{1,0:T(8,128)(2,1)}, bf16[512,3072]{1,0:T(8,128)(2,1)}) custom-call(bf16[6,2048,512]{2,1,0:T(8,128)(2,1)S(1)} %get-tuple-element.8.a, bf16[3072,512]{1,0:T(8,128)(2,1)S(1)} %get-tuple-element.9.g, bf16[3072,512]{1,0:T(8,128)(2,1)S(1)} %get-tuple-element.10.u, ...), custom_call_target="tpu_custom_call" | custom-call | tf_op jit(solution)/shard_map/write_out/pallas_call | solution.py:360

commit v5 on v4

--- a/solution.py
+++ b/solution.py
@@ -230,6 +230,8 @@
             w = columns_of(p, 1 - core)
             s0[sl, p] = term(r, w).astype(jnp.bfloat16)
             reduce_copy(0, t, p).start()
+    def own_terms(t):
+        r = pl.ds(pl.multiple_of(t * R, R), R)
         await_tiles(t, 3)
         for p in range(3):
             w = columns_of(p, core)
@@ -268,13 +270,17 @@
         def _():
             weight_grads(2 * (t - CHUNKS))
 
+        @pl.when(t < CHUNKS)
+        def _():
+            terms(t)
+
         live(t, LAGS[1], lambda k: reduce_step(2, k))
         live(t, LAGS[2], lambda k: reduce_step(3, k))
         live(t, LAGS[3], finish_step)
 
         @pl.when(t < CHUNKS)
         def _():
-            terms(t)
+            own_terms(t)
             reduce_step(1, t)
 
         live(t, LAGS[4], lambda k: gather_step(1, k))
@@ -291,6 +297,7 @@
         down_half(h).wait()
     hidden_grads(0)
     terms(0)
+    own_terms(0)
     reduce_step(1, 0)
     end = CHUNKS - 1 + LAGS[5]
     lax.fori_loop(1, end, step, 0)

time: 102 us -> 102 us (level)
  no operation moved by 1% of the time
where the time goes in v5:
time: 102 us
  Pallas kernels  101 us (99%)
    pallas_call x1, Pallas kernels, step(): pl.pallas_call(kernel, out_shape=(V((6, rows, C), bf), V((width, ff), bf)...  93.5 us
    pallas_call x1, Pallas kernels, step(): pl.pallas_call(write_out, out_shape=(jax.ShapeDtypeStruct((rows, width),...  7.54 us

profile of v5, /device:TPU:0, one launch (start us, length us, event | category | flops | bytes accessed | tf_op | source)
XLA Modules:
  0.0 101.7 jit_solution(6470918663615030278)
XLA Ops:
  0.6 93.5 %mlp_grads.1 = (bf16[6,2048,512]{2,1,0:T(8,128)(2,1)S(1)}, bf16[3072,512]{1,0:T(8,128)(2,1)S(1)}, bf16[3072,512]{1,0:T(8,128)(2,1)S(1)}, bf16[512,3072]{1,0:T(8,128)(2,1)S(1)}) custom-call(bf16[2048,3072]{1,0:T(8,128)(2,1)} %x.1, bf16[2048,3072]{1,0:T(8,128)(2,1)} %dy.1, bf16[2048,512]{1,0:T(8,128)(2,1)} %gate.1, bf16[2048,512]{1,0:T(8,128)(2,1)} %up.1, ...), custom_call_target="tpu_custom_call" | custom-call | flops 38654705664 | bytes 60000000 | tf_op jit(solution)/shard_map/mlp_grads/pallas_call | solution.py:347
  94.2 7.5 %write_out.1 = (bf16[2048,3072]{1,0:T(8,128)(2,1)}, bf16[3072,512]{1,0:T(8,128)(2,1)}, bf16[3072,512]{1,0:T(8,128)(2,1)}, bf16[512,3072]{1,0:T(8,128)(2,1)}) custom-call(bf16[6,2048,512]{2,1,0:T(8,128)(2,1)S(1)} %get-tuple-element.8.a, bf16[3072,512]{1,0:T(8,128)(2,1)S(1)} %get-tuple-element.9.g, bf16[3072,512]{1,0:T(8,128)(2,1)S(1)} %get-tuple-element.10.u, ...), custom_call_target="tpu_custom_call" | custom-call | tf_op jit(solution)/shard_map/write_out/pallas_call | solution.py:367
